TPU v7x, 256 devices: a whole 4x4x8 slice. The times are simulated.
256 devices in a mesh: gx: 16 (over z, core), gy: 4 (over x), gz: 4 (over y).
Axes of the slice: x: 4, y: 4, z: 8, core: 2. Of those that a mesh axis runs over, the one named last changes fastest.
Arguments:
- block_values: bfloat16 [4, 64, 4, 6, 128, 128], P('gy', 'gx', 'gz'), as said below
- block_cols: int32 [4, 64, 4, 6], P('gy', 'gx', 'gz'), may hold values from 0 to 63, as said below
Outputs:
- purified: float32 [2048, 32768], P(('gx', 'gy'), 'gz')
Inputs may be any that keep to these rules, and one draw needn't show every extreme that they name: block_cols[a, s, b, :] holds 6 distinct tile columns of panel b at which tile row a * 64 + s of P is nonzero; every tile column of a panel is listed by exactly 6 tile rows of each slab; the pattern is symmetric: tile (i, j) is listed exactly when tile (j, i) is. `block_values`: P is symmetric: the tile listed at (i, j) is the transpose of the tile listed at (j, i), and diagonal tiles are symmetric.
All inputs are finite; a program needn't handle non-finite values.
Results may differ from a plain program's by a relative error of at most 0.0033.
Values may be sent and summed in bfloat16 or wider, within the bound.
A program may use at most 128 MiB of HBM per device.

v0:
```python
import jax
import jax.numpy as jnp
from jax import lax
from jax.sharding import PartitionSpec as P

WIN = 1


def picked_2(x, axis, root):
    return lax.dynamic_index_in_dim(lax.all_gather(x, axis), root, 0, keepdims=False)


def in_blocks(x, dim, length):
    lengths = x.shape
    tiles = x.reshape(*lengths[:dim], length, lengths[dim] // length, *lengths[dim + 1 :])
    return jnp.moveaxis(tiles, dim, 0)


def sent_and_summed(x, axis, dim):
    tiles = in_blocks(x, dim, lax.axis_size(axis))
    arrived = lax.all_to_all(tiles, axis, split_axis=0, concat_axis=0, tiled=True)
    return arrived.astype(jnp.float32).sum(axis=0)


def densify(left_tiles, left_columns, slab_tiles):
    onehot = (
        left_columns[:, :, None] == jnp.arange(slab_tiles, dtype=jnp.int32)[None, None, :]
    ).astype(jnp.bfloat16)
    densified = jnp.einsum("wkj,wkyx->wyjx", onehot, left_tiles, preferred_element_type=jnp.float32)
    tile_size = left_tiles.shape[2]
    return densified.astype(jnp.bfloat16).reshape(
        left_tiles.shape[0] * tile_size, slab_tiles, tile_size
    )


def product_one(left_panel, panel_tiles, panel_columns):
    summed = jnp.zeros(
        (left_panel.shape[0], panel_tiles.shape[0], panel_tiles.shape[2]), jnp.float32
    )
    for column_slot in range(panel_tiles.shape[1]):
        picked = jnp.take(left_panel, panel_columns[:, column_slot], axis=1)
        summed = summed + jnp.einsum(
            "rix,iyx->riy", picked, panel_tiles[:, column_slot], preferred_element_type=jnp.float32
        )
    return summed


def product_two(rounded, panel_tiles, panel_columns, panel_width):
    summed = jnp.zeros((rounded.shape[0], panel_width, panel_tiles.shape[3]), jnp.float32)
    for column_slot in range(panel_tiles.shape[1]):
        product = jnp.einsum(
            "rix,ixy->riy", rounded, panel_tiles[:, column_slot], preferred_element_type=jnp.float32
        )
        summed = summed.at[:, panel_columns[:, column_slot], :].add(product)
    return summed


def local(block_values, block_cols):
    tiles_here = block_values[0, :, 0]
    columns_here = block_cols[0, :, 0]
    tile_size = tiles_here.shape[2]
    slab_tiles = tiles_here.shape[0] * lax.axis_size("gx")
    left_tiles, left_columns = (
        picked_2(tiles_here[:WIN], "gy", 0),
        picked_2(columns_here[:WIN], "gy", 0),
    )
    left_panel = densify(left_tiles, left_columns, slab_tiles)
    height = left_panel.shape[0]
    on_diagonal = (lax.axis_index("gy") == lax.axis_index("gz")).astype(jnp.float32)
    panel_tiles, panel_columns = (
        lax.all_gather(tiles_here, "gx", axis=0, tiled=True),
        lax.all_gather(columns_here, "gx", axis=0, tiled=True),
    )
    partial_square = product_one(left_panel, panel_tiles, panel_columns)
    partial_square = partial_square.reshape(height, slab_tiles * tile_size)
    square = lax.psum(partial_square, "gz")
    square_low = square.astype(jnp.bfloat16).reshape(height, slab_tiles, tile_size)
    applied = product_two(square_low, panel_tiles, panel_columns, slab_tiles).reshape(
        height // lax.axis_size("gy") * lax.axis_size("gy"), slab_tiles * tile_size
    )
    return sent_and_summed(
        (3.0 * on_diagonal * square - 2.0 * applied).astype(jnp.bfloat16), "gy", 0
    )


def solution(mesh):
    in_specs = (P("gy", "gx", "gz", None, None, None), P("gy", "gx", "gz", None))
    out_specs = P(("gx", "gy"), "gz")
    return jax.shard_map(local, mesh=mesh, in_specs=in_specs, out_specs=out_specs, check_vma=False)
```

profile of v0, /device:TPU:32, one launch (start us, length us, event | category | flops | bytes accessed | tf_op | source)
XLA Modules:
  0.0 381.8 jit_solution(5912386459244780532)
XLA Ops:
  6.5 0.0 slice-start.3
  6.5 0.0 slice-start.4
  6.5 0.0 all-gather.6.cloned.1.call-start
  6.5 2.2 copy.30
  8.7 0.0 all-gather.6.cloned.1.call-update
  8.7 0.0 all-reduce.2.cloned.1.call-start
  8.8 0.0 slice-done.4
  8.8 9.7 %all-gather = s32[4,1,1,6]{3,2,1,0:T(1,128)S(1)} all-gather(s32[1,1,1,6]{3,2,1,0:T(1,128)S(1)} %slice-done.4), channel_id=2, replica_groups=mesh['gx'=16,'gy'=4,'gz'=4] {'gy'}, dimensions={0}, use_global_device_ids=true | all-gather | bytes 120 | tf_op jit(solution)/shard_map/all_gather | solution.py:10
  18.5 0.0 slice-done.3
  18.5 13.3 %all-gather.1 = bf16[4,1,1,6,128,128]{5,4,3,2,1,0:T(8,128)(2,1)S(1)} all-gather(bf16[1,1,1,6,128,128]{5,4,3,2,1,0:T(8,128)(2,1)S(1)} %slice-done.3), channel_id=3, replica_groups=mesh['gx'=16,'gy'=4,'gz'=4] {'gy'}, dimensions={0}, use_global_device_ids=true | all-gather | bytes 983040 | tf_op jit(solution)/shard_map/all_gather | solution.py:10
  31.8 0.8 convert_bitcast_fusion
  32.7 0.0 copy-start.5
  32.7 1.4 copy.29
  34.0 0.0 copy-done.5
  34.1 18.6 %all-gather.2 = s32[1,64,1,6]{3,2,0,1:T(1,128)S(1)} all-gather(s32[1,4,1,6]{3,2,0,1:T(1,128)S(1)} %bitcast.101), channel_id=4, replica_groups=mesh['gx'=16,'gy'=4,'gz'=4] {'gx'}, dimensions={1}, use_global_device_ids=true | all-gather | bytes 1632 | tf_op jit(solution)/shard_map/all_gather | solution.py:72
  52.7 0.4 fusion.41
  53.1 2.2 gather_fusion
  55.3 2.1 gather_fusion.4
  57.4 2.2 gather_fusion.3
  59.6 2.1 gather_fusion.2
  61.7 2.2 gather_fusion.1
  63.9 2.1 gather_fusion.5
  66.1 19.6 %all-gather.6.cloned.1.call-done = bf16[1,64,1,6,128,128]{5,4,1,3,2,0:T(8,128)(2,1)} async-done(((bf16[1,4,1,6,128,128]{5,4,1,3,2,0:T(8,128)(2,1)}), bf16[1,64,1,6,128,128]{5,4,1,3,2,0:T(8,128)(2,1)}) %all-gather.6.cloned.1.call-update) | async-done | bytes 12582928 | tf_op jit(solution)/shard_map/all_gather | solution.py:71
  85.7 0.0 copy-start
  85.7 6.2 %fusion.10 = f32[64,128,128]{1,2,0:T(8,128)} fusion(bf16[64,128,128]{2,1,0:T(8,128)(2,1)} %gather_fusion, pred[64]{0:T(512)(128)(4,1)S(1)} %get-tuple-element.29, bf16[64,6,128,128]{3,2,0,1:T(8,128)(2,1)} %bitcast.84), kind=kOutput, calls=%fused_computation.31 | convolution fusion | flops 269484032 | bytes 8388672 | tf_op jit(solution)/shard_map/rix,iyx->riy/dot_general | solution.py:42
  91.8 0.0 copy-start.1
  91.8 6.0 %fusion.2 = f32[64,128,128]{1,2,0:T(8,128)} fusion(bf16[64,128,128]{2,1,0:T(8,128)(2,1)} %gather_fusion.4, pred[64]{0:T(512)(128)(4,1)S(1)} %get-tuple-element.25, bf16[64,6,128,128]{3,2,0,1:T(8,128)(2,1)} %bitcast.85), kind=kOutput, calls=%fused_computation.23 | convolution fusion | flops 269484032 | bytes 8388672 | tf_op jit(solution)/shard_map/rix,iyx->riy/dot_general | solution.py:42
  97.8 0.0 copy-done
  97.8 0.0 copy-done.1
  97.8 3.6 fusion.4
  101.5 0.0 copy-done.2
  101.5 0.0 copy-start.3
  101.5 3.6 fusion.6
  105.1 0.0 copy-done.3
  105.1 0.0 copy-start.4
  105.1 3.6 fusion.8
  108.7 0.0 copy-done.4
  108.7 10.1 %add_add_fusion = f32[64,128,128]{1,2,0:T(8,128)} fusion(f32[64,128,128]{1,2,0:T(8,128)} %fusion.2, f32[64,128,128]{1,2,0:T(8,128)} %fusion.4, f32[64,128,128]{1,2,0:T(8,128)} %fusion.6, f32[64,128,128]{1,2,0:T(8,128)} %fusion.10, f32[64,128,128]{1,2,0:T(8,128)} %fusion.8, bf16[64,128,128]{2,1,0:T(8,128)(2,1)S(1)} %copy-done.4, ...), kind=kOutput, calls=%fused_computation.15 | convolution fusion | flops 274726912 | bytes 29360640 | tf_op jit(solution)/shard_map/rix,iyx->riy/dot_general | solution.py:42
  118.8 0.0 all-reduce.2.cloned.1.call-update
  118.8 98.5 %all-reduce.2.cloned.1.call-done = f32[128,8192]{0,1:T(8,128)} async-done(((f32[128,8192]{0,1:T(8,128)}), f32[128,8192]{0,1:T(8,128)}) %all-reduce.2.cloned.1.call-update) | async-done | bytes 4194320 | tf_op jit(solution)/shard_map/psum | solution.py:76
  217.4 2.5 convert_element_type.27
  219.9 0.0 slice-start.1
  219.9 4.6 %fusion.24 = f32[64,128,128]{2,1,0:T(8,128)} fusion(bf16[128,64,128]{0,2,1:T(8,128)(2,1)S(1)} %bitcast.78, bf16[64,6,128,128]{3,2,0,1:T(8,128)(2,1)} %bitcast.86), kind=kOutput, calls=%fused_computation.47 | convolution fusion | flops 268435456 | bytes 8388608 | tf_op jit(solution)/shard_map/rix,ixy->riy/dot_general | solution.py:51
  224.5 4.6 %fusion.25 = f32[64,128,128]{2,1,0:T(8,128)} fusion(bf16[128,64,128]{0,2,1:T(8,128)(2,1)S(1)} %bitcast.79, bf16[64,6,128,128]{3,2,0,1:T(8,128)(2,1)} %bitcast.87), kind=kOutput, calls=%fused_computation.48 | convolution fusion | flops 268435456 | bytes 8388608 | tf_op jit(solution)/shard_map/rix,ixy->riy/dot_general | solution.py:51
  229.1 0.0 slice-done
  229.1 0.0 slice-done.1
  229.1 0.0 slice-done.2
  229.1 2.8 fusion.26
  231.9 2.8 fusion.27
  234.7 2.8 fusion.28
  237.5 2.8 fusion.29
  240.3 2.5 broadcast_in_dim.11
  242.8 13.7 %scatter_fusion = f32[128,64,128]{2,0,1:T(8,128)} fusion(f32[128,64,128]{2,0,1:T(8,128)} %broadcast_in_dim.11, s32[64]{0:T(128)S(1)} %get-tuple-element.7, f32[64,128,128]{2,1,0:T(8,128)} %fusion.24), kind=kCustom, calls=%fused_computation.6 | custom fusion | flops 1048576 | bytes 12583168 | tf_op jit(solution)/shard_map/scatter-add | solution.py:54
  256.5 13.7 %scatter_fusion.1 = f32[128,64,128]{2,0,1:T(8,128)} fusion(f32[128,64,128]{2,0,1:T(8,128)} %scatter_fusion, s32[64]{0:T(128)S(1)} %get-tuple-element.8, f32[64,128,128]{2,1,0:T(8,128)} %fusion.25), kind=kCustom, calls=%fused_computation.7 | custom fusion | flops 1048576 | bytes 12583168 | tf_op jit(solution)/shard_map/scatter-add | solution.py:54
  270.2 13.7 %scatter_fusion.2 = f32[128,64,128]{2,0,1:T(8,128)} fusion(f32[128,64,128]{2,0,1:T(8,128)} %scatter_fusion.1, s32[64]{0:T(128)S(1)} %get-tuple-element.9, f32[64,128,128]{2,1,0:T(8,128)} %fusion.26), kind=kCustom, calls=%fused_computation.8 | custom fusion | flops 1048576 | bytes 12583168 | tf_op jit(solution)/shard_map/scatter-add | solution.py:54
  283.9 13.6 %scatter_fusion.3 = f32[128,64,128]{2,0,1:T(8,128)} fusion(f32[128,64,128]{2,0,1:T(8,128)} %scatter_fusion.2, s32[64]{0:T(128)S(1)} %get-tuple-element.10, f32[64,128,128]{2,1,0:T(8,128)} %fusion.27), kind=kCustom, calls=%fused_computation.9 | custom fusion | flops 1048576 | bytes 12583168 | tf_op jit(solution)/shard_map/scatter-add | solution.py:54
  297.5 13.7 %scatter_fusion.4 = f32[128,64,128]{2,0,1:T(8,128)} fusion(f32[128,64,128]{2,0,1:T(8,128)} %scatter_fusion.3, s32[64]{0:T(128)S(1)} %get-tuple-element.11, f32[64,128,128]{2,1,0:T(8,128)} %fusion.28), kind=kCustom, calls=%fused_computation.10 | custom fusion | flops 1048576 | bytes 12583168 | tf_op jit(solution)/shard_map/scatter-add | solution.py:54
  311.1 13.6 %scatter_fusion.5 = f32[128,64,128]{2,0,1:T(8,128)} fusion(f32[128,64,128]{2,0,1:T(8,128)} %scatter_fusion.4, s32[64]{0:T(128)S(1)} %get-tuple-element.6, f32[64,128,128]{2,1,0:T(8,128)} %fusion.29), kind=kCustom, calls=%fused_computation.11 | custom fusion | flops 1048576 | bytes 12583168 | tf_op jit(solution)/shard_map/scatter-add | solution.py:54
  324.8 4.7 %broadcast_multiply_fusion = f32[128,64,128]{2,0,1:T(8,128)} fusion(f32[128,64,128]{2,0,1:T(8,128)} %scatter_fusion.5), kind=kLoop, calls=%fused_computation.39 | loop fusion | flops 1048576 | bytes 8388608 | tf_op jit(solution)/shard_map/mul | solution.py:82
  329.5 5.6 %copy.42 = f32[128,64,128]{0,2,1:T(8,128)} copy(f32[128,64,128]{2,0,1:T(8,128)} %broadcast_multiply_fusion) | data formatting | bytes 8388608 | tf_op jit(solution)/shard_map/mul | solution.py:82
  335.1 5.2 %fusion = bf16[128,8192]{0,1:T(8,128)(2,1)} fusion(f32[128,64,128]{0,2,1:T(8,128)} %copy.42, f32[128,8192]{0,1:T(8,128)} %all-reduce.2.cloned.1.call-done, f32[]{:T(128)S(6)} %mul_shard_map.3), kind=kLoop, calls=%fused_computation.13 | loop fusion | flops 3145728 | bytes 10485764 | tf_op jit(solution)/shard_map/convert_element_type | solution.py:82
  340.3 2.9 copy.43
  343.3 30.4 %all_to_all.5 = bf16[4,32,8192]{2,1,0:T(8,128)(2,1)S(1)} all-to-all(bf16[4,32,8192]{2,1,0:T(8,128)(2,1)S(1)} %bitcast.99), channel_id=1, replica_groups=mesh['gx'=16,'gy'=4,'gz'=4] {'gy'}, dimensions={0} | all-to-all | bytes 4194304 | tf_op jit(solution)/shard_map/all_to_all | solution.py:21
  373.6 1.3 convert_reduce_fusion
  (18 shorter events, 0.1 us)
Async XLA Ops:
  6.5 12.0 %slice-start.3 = ((bf16[1,4,1,6,128,128]{5,4,3,2,1,0:T(8,128)(2,1)}), bf16[1,1,1,6,128,128]{5,4,3,2,1,0:T(8,128)(2,1)S(1)}, s32[]{:S(2)}) async-start(bf16[1,4,1,6,128,128]{5,4,3,2,1,0:T(8,128)(2,1)} %param.4), calls=%async_computation.6 | async-start | bytes 393216 | tf_op jit(solution)/shard_map/slice | solution.py:64
  6.5 2.2 slice-start.4
  6.5 79.1 %all-gather.6.cloned.1.call-start = ((), (), s32[]{:S(2)}) async-start(), calls=%async_computation.2 | async-start | bytes 13369344 | tf_op jit(solution)/shard_map/all_gather | solution.py:71
  8.7 208.6 %all-reduce.2.cloned.1.call-start = ((), (), s32[]{:S(2)}) async-start(), calls=%async_computation.1 | async-start | bytes 8388608 | tf_op jit(solution)/shard_map/psum | solution.py:76
  32.7 1.4 copy-start.5
  85.7 12.2 %copy-start = (bf16[1,64,1,6,128,128]{5,4,1,3,2,0:T(8,128)(2,1)S(1)}, bf16[1,64,1,6,128,128]{5,4,1,3,2,0:T(8,128)(2,1)}, u32[]{:S(2)}) copy-start(bf16[1,64,1,6,128,128]{5,4,1,3,2,0:T(8,128)(2,1)} %all-gather.6.cloned.1.call-done) | copy-start | bytes 37748740
  91.8 6.0 %copy-start.1 = (bf16[64,128,128]{2,1,0:T(8,128)(2,1)S(1)}, bf16[64,128,128]{2,1,0:T(8,128)(2,1)}, u32[]{:S(2)}) copy-start(bf16[64,128,128]{2,1,0:T(8,128)(2,1)} %gather_fusion.3) | copy-start | bytes 6291460
  97.8 3.6 copy-start.2
  101.5 3.6 copy-start.3
  105.1 3.6 copy-start.4
  217.4 11.7 %slice-start = ((s8[12582912]{0:T(1024)(128)(4,1)}), s8[4194304]{0:T(1024)(128)(4,1)S(1)}, s32[]{:S(2)}) async-start(s8[12582912]{0:T(1024)(128)(4,1)} %bitcast.92), calls=%async_computation.3 | async-start | bytes 8388608
  219.9 9.2 %slice-start.1 = ((s8[12582912]{0:T(1024)(128)(4,1)}), s8[4194304]{0:T(1024)(128)(4,1)S(1)}, s32[]{:S(2)}) async-start(s8[12582912]{0:T(1024)(128)(4,1)} %bitcast.92), calls=%async_computation.4 | async-start | bytes 8388608
  224.5 4.6 %slice-start.2 = ((s8[12582912]{0:T(1024)(128)(4,1)}), s8[4194304]{0:T(1024)(128)(4,1)S(1)}, s32[]{:S(2)}) async-start(s8[12582912]{0:T(1024)(128)(4,1)} %bitcast.92), calls=%async_computation.5 | async-start | bytes 8388608
Sparse Core Ops, SparseCore 0:
  9.2 76.4 all-gather.5
  118.9 98.3 all-reduce.1
where the time goes:
time: 383 us; the launch traced here: 382 us
  waiting for transfers between devices  118 us (31%)
  other arithmetic  96.3 us (25%)
  blocking collectives  72 us (19%)
  matrix products  54.3 us (14%)
  local copies, waits for them, and re-layouts  27.4 us (7%)
  between operations  13.5 us (4%)
    psum x1, waiting for transfers between devices, local(): square = lax.psum(partial_square, 'gz')  98.5 us
    scatter-add x6, other arithmetic, product_two(): summed = summed.at[:, panel_columns[:, column_slot], :].add(product)  82 us
    dot_general x6, matrix products, product_one(): jnp.einsum('rix,iyx->riy', picked, panel_tiles[:, column_slot], preferred...  33.1 us
    all_to_all x1, blocking collectives, sent_and_summed(): lax.all_to_all(tiles, axis, split_axis=0, concat_axis=0, tiled=True)  30.4 us
    all_gather x2, blocking collectives, picked_2(): lax.all_gather(x, axis)  23 us
    dot_general x6, matrix products, product_two(): jnp.einsum('rix,ixy->riy', rounded, panel_tiles[:, column_slot], preferre...  20.4 us
    all_gather x1, waiting for transfers between devices, local(): lax.all_gather(tiles_here, 'gx', axis=0, tiled=True)  19.6 us
    all_gather x1, blocking collectives, local(): lax.all_gather(columns_here, 'gx', axis=0, tiled=True)  18.6 us
  transfers between devices with their start and end apart: 2, of which 2 were waited for; matrix products, arithmetic and copies ran while one was open for 4% of the time, Pallas kernels for 0%

commit v1 on v0

--- a/solution.py
+++ b/solution.py
@@ -73,7 +73,11 @@
     )
     partial_square = product_one(left_panel, panel_tiles, panel_columns)
     partial_square = partial_square.reshape(height, slab_tiles * tile_size)
-    square = lax.psum(partial_square, "gz")
+    devices = lax.axis_size("gz")
+    square, reach = (partial_square, 1)
+    while reach < devices:
+        square = square + lax.ppermute(square, "gz", [(i, i ^ reach) for i in range(devices)])
+        reach = 2 * reach
     square_low = square.astype(jnp.bfloat16).reshape(height, slab_tiles, tile_size)
     applied = product_two(square_low, panel_tiles, panel_columns, slab_tiles).reshape(
         height // lax.axis_size("gy") * lax.axis_size("gy"), slab_tiles * tile_size

time: 383 us -> 480 us (1.25)
  waiting for transfers between devices: 118 us -> 200 us
  other arithmetic: 96.3 us -> 104 us
    ppermute x0 -> x2, waiting for transfers between devices: none -> 182 us  [local(): lax.ppermute(square, 'gz', [(i, i ^ reach) for i in range(devices)])]
    psum x1 -> x0, waiting for transfers between devices: 98.5 us -> none  [local(): square = lax.psum(partial_square, 'gz')]
  transfers between devices with their start and end apart: 2 -> 3, of which waited for: 2 -> 3; matrix products, arithmetic and copies ran while one was open for 4% -> 4% of each run, Pallas kernels for 0% -> 0%
where the time goes in v1:
time: 480 us; the launch traced here: 477 us
  waiting for transfers between devices  200 us (42%)
  other arithmetic  104 us (22%)
  blocking collectives  70.8 us (15%)
  matrix products  54.9 us (11%)
  local copies, waits for them, and re-layouts  29.1 us (6%)
  between operations  13.5 us (3%)
    ppermute x2, waiting for transfers between devices, local(): lax.ppermute(square, 'gz', [(i, i ^ reach) for i in range(devices)])  182 us
    scatter-add x6, other arithmetic, product_two(): summed = summed.at[:, panel_columns[:, column_slot], :].add(product)  82.2 us
    dot_general x6, matrix products, product_one(): jnp.einsum('rix,iyx->riy', picked, panel_tiles[:, column_slot], preferred...  33.1 us
    all_to_all x1, blocking collectives, sent_and_summed(): lax.all_to_all(tiles, axis, split_axis=0, concat_axis=0, tiled=True)  29.2 us
    all_gather x2, blocking collectives, picked_2(): lax.all_gather(x, axis)  23 us
    dot_general x6, matrix products, product_two(): jnp.einsum('rix,ixy->riy', rounded, panel_tiles[:, column_slot], preferre...  20.9 us
    all_gather x1, blocking collectives, local(): lax.all_gather(columns_here, 'gx', axis=0, tiled=True)  18.6 us
    all_gather x1, waiting for transfers between devices, local(): lax.all_gather(tiles_here, 'gx', axis=0, tiled=True)  18.1 us
  transfers between devices with their start and end apart: 3, of which 3 were waited for; matrix products, arithmetic and copies ran while one was open for 4% of the time, Pallas kernels for 0%

profile of v1, /device:TPU:32, one launch (start us, length us, event | category | flops | bytes accessed | tf_op | source)
XLA Modules:
  0.0 476.9 jit_solution(5308915799172064678)
XLA Ops:
  6.5 0.0 all-gather.6.cloned.1.call-start
  6.5 2.1 copy.30
  8.6 0.0 all-gather.6.cloned.1.call-update
  8.6 0.0 copy-start.5
  8.7 0.7 slice.58
  9.4 9.7 %all-gather = s32[4,1,1,6]{3,2,1,0:T(1,128)S(1)} all-gather(s32[1,1,1,6]{3,2,1,0:T(1,128)S(1)} %slice.58), channel_id=2, replica_groups=mesh['gx'=16,'gy'=4,'gz'=4] {'gy'}, dimensions={0}, use_global_device_ids=true | all-gather | bytes 120 | tf_op jit(solution)/shard_map/all_gather | solution.py:10
  19.1 0.9 slice.59
  20.0 13.3 %all-gather.1 = bf16[4,1,1,6,128,128]{5,4,3,2,1,0:T(8,128)(2,1)S(1)} all-gather(bf16[1,1,1,6,128,128]{5,4,3,2,1,0:T(8,128)(2,1)S(1)} %slice.59), channel_id=3, replica_groups=mesh['gx'=16,'gy'=4,'gz'=4] {'gy'}, dimensions={0}, use_global_device_ids=true | all-gather | bytes 983040 | tf_op jit(solution)/shard_map/all_gather | solution.py:10
  33.4 0.8 convert_bitcast_fusion
  34.2 1.4 copy.29
  35.6 0.0 copy-done.5
  35.6 18.6 %all-gather.2 = s32[1,64,1,6]{3,2,0,1:T(1,128)S(1)} all-gather(s32[1,4,1,6]{3,2,0,1:T(1,128)S(1)} %bitcast.102), channel_id=4, replica_groups=mesh['gx'=16,'gy'=4,'gz'=4] {'gx'}, dimensions={1}, use_global_device_ids=true | all-gather | bytes 1632 | tf_op jit(solution)/shard_map/all_gather | solution.py:72
  54.2 0.4 fusion.41
  54.6 2.2 gather_fusion
  56.8 2.1 gather_fusion.4
  58.9 2.2 gather_fusion.3
  61.1 2.1 gather_fusion.2
  63.2 2.2 gather_fusion.1
  65.4 2.1 gather_fusion.5
  67.6 18.1 %all-gather.6.cloned.1.call-done = bf16[1,64,1,6,128,128]{5,4,1,3,2,0:T(8,128)(2,1)} async-done(((bf16[1,4,1,6,128,128]{5,4,1,3,2,0:T(8,128)(2,1)}), bf16[1,64,1,6,128,128]{5,4,1,3,2,0:T(8,128)(2,1)}) %all-gather.6.cloned.1.call-update) | async-done | bytes 12582928 | tf_op jit(solution)/shard_map/all_gather | solution.py:71
  85.7 0.0 copy-start
  85.7 6.2 %fusion.10 = f32[64,128,128]{1,2,0:T(8,128)} fusion(bf16[64,128,128]{2,1,0:T(8,128)(2,1)} %gather_fusion, pred[64]{0:T(512)(128)(4,1)S(1)} %get-tuple-element.29, bf16[64,6,128,128]{3,2,0,1:T(8,128)(2,1)} %bitcast.85), kind=kOutput, calls=%fused_computation.31 | convolution fusion | flops 269484032 | bytes 8388672 | tf_op jit(solution)/shard_map/rix,iyx->riy/dot_general | solution.py:42
  91.8 0.0 copy-start.1
  91.8 6.0 %fusion.2 = f32[64,128,128]{1,2,0:T(8,128)} fusion(bf16[64,128,128]{2,1,0:T(8,128)(2,1)} %gather_fusion.4, pred[64]{0:T(512)(128)(4,1)S(1)} %get-tuple-element.25, bf16[64,6,128,128]{3,2,0,1:T(8,128)(2,1)} %bitcast.86), kind=kOutput, calls=%fused_computation.23 | convolution fusion | flops 269484032 | bytes 8388672 | tf_op jit(solution)/shard_map/rix,iyx->riy/dot_general | solution.py:42
  97.8 0.0 copy-done
  97.8 0.0 copy-done.1
  97.8 0.0 copy-start.2
  97.8 3.6 fusion.4
  101.4 0.0 copy-done.2
  101.5 0.0 copy-start.3
  101.5 3.6 fusion.6
  105.1 0.0 copy-done.3
  105.1 3.6 fusion.8
  108.7 0.0 copy-done.4
  108.7 10.1 %add_add_fusion = f32[64,128,128]{1,2,0:T(8,128)} fusion(f32[64,128,128]{1,2,0:T(8,128)} %fusion.2, f32[64,128,128]{1,2,0:T(8,128)} %fusion.4, f32[64,128,128]{1,2,0:T(8,128)} %fusion.6, f32[64,128,128]{1,2,0:T(8,128)} %fusion.10, f32[64,128,128]{1,2,0:T(8,128)} %fusion.8, bf16[64,128,128]{2,1,0:T(8,128)(2,1)S(1)} %copy-done.4, ...), kind=kOutput, calls=%fused_computation.15 | convolution fusion | flops 274726912 | bytes 29360640 | tf_op jit(solution)/shard_map/rix,iyx->riy/dot_general | solution.py:42
  118.8 1.5 collective-permute-start
  120.3 91.4 %collective-permute-done = f32[128,8192]{0,1:T(8,128)S(1)} collective-permute-done((f32[128,8192]{0,1:T(8,128)}, f32[128,8192]{0,1:T(8,128)S(1)}, u32[]{:S(2)}, u32[]{:S(2)}) %collective-permute-start) | collective-permute-done | bytes 4194336 | tf_op jit(solution)/shard_map/ppermute | solution.py:79
  211.7 4.7 bitcast_add_fusion
  216.4 3.0 collective-permute-start.1
  219.4 90.7 %collective-permute-done.1 = f32[128,8192]{0,1:T(8,128)} collective-permute-done((f32[128,8192]{0,1:T(8,128)}, f32[128,8192]{0,1:T(8,128)}, u32[]{:S(2)}, u32[]{:S(2)}) %collective-permute-start.1) | collective-permute-done | bytes 4194336 | tf_op jit(solution)/shard_map/ppermute | solution.py:79
  310.1 4.0 add_convert_fusion
  314.1 0.0 slice-start.2
  314.1 5.2 %fusion.24 = f32[64,128,128]{2,1,0:T(8,128)} fusion(bf16[128,64,128]{0,2,1:T(8,128)(2,1)S(1)} %bitcast.79, bf16[64,6,128,128]{3,2,0,1:T(8,128)(2,1)} %bitcast.87), kind=kOutput, calls=%fused_computation.47 | convolution fusion | flops 268435456 | bytes 8388608 | tf_op jit(solution)/shard_map/rix,ixy->riy/dot_general | solution.py:51
  319.3 4.4 fusion.25
  323.8 0.0 slice-done
  323.8 0.0 slice-done.1
  323.8 0.0 slice-done.2
  323.8 2.8 fusion.26
  326.6 2.8 fusion.27
  329.4 2.8 fusion.28
  332.3 2.8 fusion.29
  335.1 2.6 broadcast_in_dim.11
  337.6 13.9 %scatter_fusion = f32[128,64,128]{2,0,1:T(8,128)} fusion(f32[128,64,128]{2,0,1:T(8,128)} %broadcast_in_dim.11, s32[64]{0:T(128)S(1)} %get-tuple-element.7, f32[64,128,128]{2,1,0:T(8,128)} %fusion.24), kind=kCustom, calls=%fused_computation.6 | custom fusion | flops 1048576 | bytes 12583168 | tf_op jit(solution)/shard_map/scatter-add | solution.py:54
  351.5 13.7 %scatter_fusion.1 = f32[128,64,128]{2,0,1:T(8,128)} fusion(f32[128,64,128]{2,0,1:T(8,128)} %scatter_fusion, s32[64]{0:T(128)S(1)} %get-tuple-element.8, f32[64,128,128]{2,1,0:T(8,128)} %fusion.25), kind=kCustom, calls=%fused_computation.7 | custom fusion | flops 1048576 | bytes 12583168 | tf_op jit(solution)/shard_map/scatter-add | solution.py:54
  365.2 13.7 %scatter_fusion.2 = f32[128,64,128]{2,0,1:T(8,128)} fusion(f32[128,64,128]{2,0,1:T(8,128)} %scatter_fusion.1, s32[64]{0:T(128)S(1)} %get-tuple-element.9, f32[64,128,128]{2,1,0:T(8,128)} %fusion.26), kind=kCustom, calls=%fused_computation.8 | custom fusion | flops 1048576 | bytes 12583168 | tf_op jit(solution)/shard_map/scatter-add | solution.py:54
  378.9 13.7 %scatter_fusion.3 = f32[128,64,128]{2,0,1:T(8,128)} fusion(f32[128,64,128]{2,0,1:T(8,128)} %scatter_fusion.2, s32[64]{0:T(128)S(1)} %get-tuple-element.10, f32[64,128,128]{2,1,0:T(8,128)} %fusion.27), kind=kCustom, calls=%fused_computation.9 | custom fusion | flops 1048576 | bytes 12583168 | tf_op jit(solution)/shard_map/scatter-add | solution.py:54
  392.6 13.6 %scatter_fusion.4 = f32[128,64,128]{2,0,1:T(8,128)} fusion(f32[128,64,128]{2,0,1:T(8,128)} %scatter_fusion.3, s32[64]{0:T(128)S(1)} %get-tuple-element.11, f32[64,128,128]{2,1,0:T(8,128)} %fusion.28), kind=kCustom, calls=%fused_computation.10 | custom fusion | flops 1048576 | bytes 12583168 | tf_op jit(solution)/shard_map/scatter-add | solution.py:54
  406.2 13.7 %scatter_fusion.5 = f32[128,64,128]{2,0,1:T(8,128)} fusion(f32[128,64,128]{2,0,1:T(8,128)} %scatter_fusion.4, s32[64]{0:T(128)S(1)} %get-tuple-element.6, f32[64,128,128]{2,1,0:T(8,128)} %fusion.29), kind=kCustom, calls=%fused_computation.11 | custom fusion | flops 1048576 | bytes 12583168 | tf_op jit(solution)/shard_map/scatter-add | solution.py:54
  419.8 4.7 broadcast_multiply_fusion
  424.6 5.6 %copy.42 = f32[128,64,128]{0,2,1:T(8,128)} copy(f32[128,64,128]{2,0,1:T(8,128)} %broadcast_multiply_fusion) | data formatting | bytes 8388608 | tf_op jit(solution)/shard_map/mul | solution.py:86
  430.2 6.5 %fusion = bf16[128,8192]{0,1:T(8,128)(2,1)} fusion(f32[128,64,128]{0,2,1:T(8,128)} %copy.42, f32[]{:T(128)S(6)} %mul_shard_map.3, f32[128,8192]{0,1:T(8,128)} %bitcast_add_fusion, f32[128,8192]{0,1:T(8,128)} %collective-permute-done.1), kind=kLoop, calls=%fused_computation.13 | loop fusion | flops 4194304 | bytes 14680068 | tf_op jit(solution)/shard_map/convert_element_type | solution.py:86
  436.7 2.9 copy.43
  439.6 29.2 %all_to_all.5 = bf16[4,32,8192]{2,1,0:T(8,128)(2,1)S(1)} all-to-all(bf16[4,32,8192]{2,1,0:T(8,128)(2,1)S(1)} %bitcast.100), channel_id=1, replica_groups=mesh['gx'=16,'gy'=4,'gz'=4] {'gy'}, dimensions={0} | all-to-all | bytes 4194304 | tf_op jit(solution)/shard_map/all_to_all | solution.py:21
  468.8 1.3 convert_reduce_fusion
  (18 shorter events, 0.1 us)
Async XLA Ops:
  6.5 79.1 %all-gather.6.cloned.1.call-start = ((), (), s32[]{:S(2)}) async-start(), calls=%async_computation.1 | async-start | bytes 13369344 | tf_op jit(solution)/shard_map/all_gather | solution.py:71
  8.6 26.9 %copy-start.5 = (s32[1,4,1,6]{3,2,1,0:T(1,128)S(1)}, s32[1,4,1,6]{3,2,1,0:T(1,128)}, u32[]{:S(2)}) copy-start(s32[1,4,1,6]{3,2,1,0:T(1,128)} %param.5) | copy-start | bytes 292
  85.7 12.2 %copy-start = (bf16[1,64,1,6,128,128]{5,4,1,3,2,0:T(8,128)(2,1)S(1)}, bf16[1,64,1,6,128,128]{5,4,1,3,2,0:T(8,128)(2,1)}, u32[]{:S(2)}) copy-start(bf16[1,64,1,6,128,128]{5,4,1,3,2,0:T(8,128)(2,1)} %all-gather.6.cloned.1.call-done) | copy-start | bytes 37748740
  91.8 6.0 %copy-start.1 = (bf16[64,128,128]{2,1,0:T(8,128)(2,1)S(1)}, bf16[64,128,128]{2,1,0:T(8,128)(2,1)}, u32[]{:S(2)}) copy-start(bf16[64,128,128]{2,1,0:T(8,128)(2,1)} %gather_fusion.3) | copy-start | bytes 6291460
  97.8 3.6 copy-start.2
  101.5 3.6 copy-start.3
  105.1 3.6 copy-start.4
  118.8 92.9 %collective-permute-start = (f32[128,8192]{0,1:T(8,128)}, f32[128,8192]{0,1:T(8,128)S(1)}, u32[]{:S(2)}, u32[]{:S(2)}) collective-permute-start(f32[128,8192]{0,1:T(8,128)} %bitcast.99), channel_id=1, source_target_pairs={{0,1},{1,0},{2,3},{3,2},{4,5},{5,4},{6,7},{7,6},{8,9},{9,8},{10,11... | collective-permute-start | bytes 12582920 | tf_op jit(solution)/shard_map/ppermute | solution.py:79
  216.4 93.7 %collective-permute-start.1 = (f32[128,8192]{0,1:T(8,128)}, f32[128,8192]{0,1:T(8,128)}, u32[]{:S(2)}, u32[]{:S(2)}) collective-permute-start(f32[128,8192]{0,1:T(8,128)} %bitcast_add_fusion), channel_id=1, source_target_pairs={{0,2},{1,3},{2,0},{3,1},{4,6},{5,7},{6,4},{7,5},{8,10},{9,11},{10,... | collective-permute-start | bytes 12582920 | tf_op jit(solution)/shard_map/ppermute | solution.py:79
  310.1 13.7 %slice-start = ((s8[12582912]{0:T(1024)(128)(4,1)}), s8[4194304]{0:T(1024)(128)(4,1)S(1)}, s32[]{:S(2)}) async-start(s8[12582912]{0:T(1024)(128)(4,1)} %bitcast.93), calls=%async_computation.2 | async-start | bytes 8388608
  310.1 13.7 %slice-start.1 = ((s8[12582912]{0:T(1024)(128)(4,1)}), s8[4194304]{0:T(1024)(128)(4,1)S(1)}, s32[]{:S(2)}) async-start(s8[12582912]{0:T(1024)(128)(4,1)} %bitcast.93), calls=%async_computation.3 | async-start | bytes 8388608
  314.1 9.7 %slice-start.2 = ((s8[12582912]{0:T(1024)(128)(4,1)}), s8[4194304]{0:T(1024)(128)(4,1)S(1)}, s32[]{:S(2)}) async-start(s8[12582912]{0:T(1024)(128)(4,1)} %bitcast.93), calls=%async_computation.4 | async-start | bytes 8388608
Sparse Core Ops, SparseCore 0:
  9.2 76.4 all-gather.5
